TPU v7x, 32 devices: a whole 2x2x4 slice. The times are simulated.
32 devices in a mesh: gx: 4 (over y, core), gy: 4 (over z), gz: 2 (over x).
Axes of the slice: x: 2, y: 2, z: 4, core: 2. Of those that a mesh axis runs over, the one named last changes fastest.
Arguments:
- a_vals: float32 [4, 8, 2, 6, 128, 128], P('gy', 'gx', 'gz'), may hold values from -0.25 to 0.25
- a_cols: int32 [4, 8, 2, 6], P('gy', 'gx', 'gz'), may hold values from 0 to 15, as said below
- a_count: int32 [4, 8, 2], P('gy', 'gx', 'gz'), may hold values from 1 to 6, as said below
- p_vals: float32 [2, 16, 4, 1, 128, 128], P('gz', 'gy', 'gx'), may hold values from -6 to 6
- p_cols: int32 [2, 16, 4, 1], P('gz', 'gy', 'gx'), may hold values from 0 to 1, as said below
- p_count: int32 [2, 16, 4], P('gz', 'gy', 'gx'), may hold values from 0 to 1, as said below
Outputs:
- c_tiles: float32 [4096, 1024], P(('gy', 'gz'), 'gx')
Inputs may be any that keep to these rules, and one draw needn't show every extreme that they name: `a_cols`: inner tile indices of one block row and slice are distinct across its 6 slots. Slots 0 to a_count - 1 are live; the block rows of every device include one with all 6 slots live. `p_cols`: column tiles of one block row and group are distinct across its 1 slots. Slots 0 to p_count - 1 are live; the block rows of every device include one with all 1 slots live.
All inputs are finite; a program needn't handle non-finite values.
Results may differ from a plain program's by a relative error of at most 0.0003.
Values sent between devices are 32-bit elements; how exact they have to be, the bound alone decides.
A program may use at most 128 MiB of HBM per device.

v0:
```python
import jax
import jax.numpy as jnp
from jax import lax
from jax.sharding import PartitionSpec as P

COLS_DEV = 2


HIGHEST = lax.Precision.HIGHEST


def placement_weights(counts, columns, column_tiles):
    slot_total = columns.shape[-1]
    alive_slots = jnp.arange(slot_total, dtype=jnp.int32) < counts[..., None]
    matches = columns[..., None] == jnp.arange(column_tiles, dtype=jnp.int32)
    return (alive_slots[..., None] & matches).astype(jnp.float32)


def body(a_vals, a_cols, a_count, p_vals, p_cols, p_count):
    tile_size = a_vals.shape[-1]
    slots_a = a_vals.shape[3]
    alive_a = jnp.arange(slots_a, dtype=jnp.int32) < a_count[..., None]
    a_masked = jnp.where(alive_a[..., None, None], a_vals, 0.0)
    weights = placement_weights(p_count, p_cols, COLS_DEV)
    strip_width = COLS_DEV * tile_size
    values_all, weights_all = (
        lax.all_gather(p_vals, "gy", axis=1, tiled=True),
        lax.all_gather(weights, "gy", axis=1, tiled=True),
    )
    values_all = values_all[0, :, 0]
    weights_all = weights_all[0, :, 0]
    tile_part = lax.all_gather(a_masked, "gx", axis=1, tiled=True)
    columns = lax.all_gather(a_cols, "gx", axis=1, tiled=True)
    row_count = tile_part.shape[1]
    block_tile_part = tile_part[0, :, 0]
    indices = columns[0, :, 0]
    chosen = values_all[indices]
    product = jnp.einsum("nsij,nspjk->nspik", block_tile_part, chosen, precision=HIGHEST)
    placed = jnp.einsum("nspc,nspik->nick", weights_all[indices], product, precision=HIGHEST)
    block = placed.reshape(placed.shape[0], tile_size, strip_width).reshape(
        row_count * tile_size, strip_width
    )
    return lax.psum_scatter(block, "gz", scatter_dimension=0, tiled=True)


def solution(mesh):
    placed = (
        P("gy", "gx", "gz", None, None, None),
        P("gy", "gx", "gz", None),
        P("gy", "gx", "gz"),
        P("gz", "gy", "gx", None, None, None),
        P("gz", "gy", "gx", None),
        P("gz", "gy", "gx"),
    )
    return jax.shard_map(
        body, mesh=mesh, in_specs=placed, out_specs=P(("gy", "gz"), "gx"), check_vma=False
    )
```

profile of v0, /device:TPU:0, one launch (start us, length us, event | category | flops | bytes accessed | tf_op | source)
XLA Modules:
  0.0 114.0 jit_solution(6142502463794559515)
XLA Ops:
  6.5 0.0 all-gather.3.cloned.1.call-start
  6.5 0.7 all-gather.3.cloned.1.call-update
  7.3 0.0 all-gather.5.cloned.1.call-start
  7.3 0.7 iota_compare_fusion
  8.0 2.1 %bitcast_select_fusion = f32[1,2,1,6,128,128]{5,4,3,2,0,1:T(8,128)} fusion(f32[1,2,1,6,128,128]{5,4,3,2,1,0:T(8,128)} %param.6, pred[2,6]{1,0:T(4,128)(4,1)S(1)} %iota_compare_fusion), kind=kLoop, calls=%fused_computation.6 | loop fusion | flops 196608 | bytes 1572876 | tf_op jit(solution)/shard_map/jit(_where)/select_n | solution.py:23
  10.2 0.0 all-gather.5.cloned.1.call-update
  10.2 0.0 reduce-scatter.2.cloned.1.call-start
  10.2 0.7 compare_bitcast_fusion
  10.9 0.7 and_convert_fusion
  11.6 13.7 %all_gather.15 = f32[1,16,1,1,2]{4,3,2,0,1:T(1,128)S(1)} all-gather(f32[1,4,1,1,2]{4,3,2,0,1:T(1,128)S(1)} %and_convert_fusion), channel_id=1, replica_groups=mesh['gx'=4,'gy'=4,'gz'=2] {'gy'}, dimensions={1}, use_global_device_ids=true | all-gather | bytes 160 | tf_op jit(solution)/shard_map/all_gather | solution.py:28
  25.4 5.3 %all_gather.13 = s32[1,8,1,6]{3,2,0,1:T(1,128)S(1)} all-gather(s32[1,2,1,6]{3,2,0,1:T(1,128)} %bitcast.44), channel_id=1, replica_groups=mesh['gx'=4,'gy'=4,'gz'=2] {'gx'}, dimensions={1}, use_global_device_ids=true | all-gather | bytes 240 | tf_op jit(solution)/shard_map/all_gather | solution.py:33
  30.6 0.1 copy.25
  30.7 0.1 copy.26
  30.8 0.1 reshape.152
  30.9 0.6 gather_fusion.1
  31.5 0.1 copy.31
  31.6 0.1 reshape.147
  31.6 8.1 %all-gather.3.cloned.1.call-done = f32[1,16,1,1,128,128]{5,4,3,2,0,1:T(8,128)} async-done(((f32[1,4,1,1,128,128]{5,4,3,2,0,1:T(8,128)}), f32[1,16,1,1,128,128]{5,4,3,2,0,1:T(8,128)}) %all-gather.3.cloned.1.call-update) | async-done | bytes 1048592 | tf_op jit(solution)/shard_map/all_gather | solution.py:27
  39.7 3.7 %gather_fusion = f32[48,128,128]{2,1,0:T(8,128)} fusion(f32[16,128,128]{2,1,0:T(8,128)} %bitcast.38, s32[1024]{0:T(1024)S(1)} %pad_clamp_fusion), kind=kCustom, calls=%fused_computation | custom fusion | bytes 6291648 | tf_op jit(solution)/shard_map/gather | solution.py:37
  43.4 25.8 %all-gather.5.cloned.1.call-done = f32[1,8,1,6,128,128]{5,4,3,2,0,1:T(8,128)} async-done(((f32[1,2,1,6,128,128]{5,4,3,2,0,1:T(8,128)}), f32[1,8,1,6,128,128]{5,4,3,2,0,1:T(8,128)}) %all-gather.5.cloned.1.call-update) | async-done | bytes 3145744 | tf_op jit(solution)/shard_map/all_gather | solution.py:32
  69.1 7.2 %fusion.2 = f32[8,6,128,128]{2,3,1,0:T(8,128)S(1)} fusion(f32[8,6,128,128]{3,2,1,0:T(8,128)} %bitcast.37, f32[1,8,1,6,128,128]{5,4,3,2,0,1:T(8,128)} %all-gather.5.cloned.1.call-done), kind=kOutput, calls=%fused_computation.4 | convolution fusion | flops 1207959552 | bytes 9437184 | tf_op jit(solution)/shard_map/nsij,nspjk->nspik/dot_general | solution.py:38
  76.4 3.6 %copy.32 = f32[8,6,128,128]{3,1,2,0:T(8,128)} copy(f32[8,6,128,128]{2,3,1,0:T(8,128)S(1)} %fusion.2) | data formatting | bytes 6291456 | tf_op jit(solution)/shard_map/reshape.8
  80.0 5.9 %fusion.5 = f32[8,128,128,2]{2,3,1,0:T(2,128)S(1)} fusion(f32[8,6,128,128]{3,1,2,0:T(8,128)} %copy.32, f32[8,6,2,1]{1,0,2,3:T(8,128)S(1)} %bitcast.43), kind=kOutput, calls=%fused_computation.8 | convolution fusion | flops 18874368 | bytes 4194688 | tf_op jit(solution)/shard_map/nspc,nspik->nick/dot_general | solution.py:39
  85.9 1.0 copy.43
  86.9 0.0 reduce-scatter.2.cloned.1.call-update
  86.9 20.5 %reduce-scatter.2.cloned.1.call-done = f32[512,256]{1,0:T(8,128)} async-done(((f32[1024,256]{1,0:T(8,128)}), f32[512,256]{1,0:T(8,128)}) %reduce-scatter.2.cloned.1.call-update) | async-done | bytes 524304 | tf_op jit(solution)/shard_map/reduce_scatter | solution.py:43
  (2 shorter events, 0.0 us)
Async XLA Ops:
  6.5 33.2 %all-gather.3.cloned.1.call-start = ((), (), s32[]{:S(2)}) async-start(), calls=%async_computation.1 | async-start | bytes 1310720 | tf_op jit(solution)/shard_map/all_gather | solution.py:27
  7.3 61.9 %all-gather.5.cloned.1.call-start = ((), (), s32[]{:S(2)}) async-start(), calls=%async_computation.2 | async-start | bytes 3932160 | tf_op jit(solution)/shard_map/all_gather | solution.py:32
  10.2 97.3 %reduce-scatter.2.cloned.1.call-start = ((), (), s32[]{:S(2)}) async-start(), calls=%async_computation.3 | async-start | bytes 1572864 | tf_op jit(solution)/shard_map/reduce_scatter | solution.py:43
Sparse Core Ops, SparseCore 0:
  8.9 30.7 all-gather.2
  41.3 27.8 all-gather.4
  87.1 20.3 reduce-scatter.1
where the time goes:
time: 114 us
  waiting for transfers between devices  55.1 us (48%)
  blocking collectives  19 us (17%)
  matrix products  13.1 us (11%)
  between operations  13.1 us (11%)
  local copies, waits for them, and re-layouts  9.29 us (8%)
  other arithmetic  4.27 us (4%)
    all_gather x1, waiting for transfers between devices, body(): tile_part = lax.all_gather(a_masked, 'gx', axis=1, tiled=True)  25.8 us
    reduce_scatter x1, waiting for transfers between devices, body(): return lax.psum_scatter(block, 'gz', scatter_dimension=0, tiled=True)  20.5 us
    all_gather x1, blocking collectives, body(): lax.all_gather(weights, 'gy', axis=1, tiled=True)  13.7 us
    all_gather x1, waiting for transfers between devices, body(): lax.all_gather(p_vals, 'gy', axis=1, tiled=True)  8.07 us
    dot_general x1, matrix products, body(): jnp.einsum('nsij,nspjk->nspik', block_tile_part, chosen, precision=HIGHEST)  7.22 us
    dot_general x1, matrix products, body(): jnp.einsum('nspc,nspik->nick', weights_all[indices], product, precision=H...  5.89 us
    all_gather x1, blocking collectives, body(): columns = lax.all_gather(a_cols, 'gx', axis=1, tiled=True)  5.26 us
    another operation x2, local copies, waits for them, and re-layouts  3.69 us
  transfers between devices with their start and end apart: 3, of which 3 were waited for; matrix products, arithmetic and copies ran while one was open for 8% of the time, Pallas kernels for 0%

commit v1 on v0

v1 whole, which is shorter than its diff:
```python
import functools

import jax
import jax.numpy as jnp
from jax import lax
from jax.experimental import pallas as pl
from jax.experimental.pallas import tpu as pltpu
from jax.sharding import PartitionSpec as P

COLS_DEV = 2
MESH = pl.DeviceIdType.MESH


def kernel(
    gx, gy, gz,
    a_ref, p_ref, m_ref, o_ref,
    a_all, p_all, ma, mp, sa, sp, p_hi, p_lo, c_send, c_recv,
    a_recv, a_sy, a_sp, a_sf, p_recv, p_send, ma_recv, ma_send, mp_recv, mp_send, s_sem,
    c_rs, c_ss,
):
    rows, slots, tile = a_ref.shape[0], a_ref.shape[1], a_ref.shape[2]
    inner, slots_p = p_ref.shape[0], p_ref.shape[1]
    rows_all = gx * rows
    rows_out = rows_all // gz
    zero_tile = gy * inner
    cuts_a = 2 if slots % 2 == 0 else 1
    cuts_p = 2 if inner % 2 == 0 else 1
    part_a, part_p = slots // cuts_a, inner // cuts_p
    me_x, me_y, me_z = lax.axis_index("gx"), lax.axis_index("gy"), lax.axis_index("gz")
    chips = gx // 2
    chip, core = me_x // 2, me_x % 2
    partner = chip * 2 + (1 - core)

    barrier = pltpu.get_barrier_semaphore()
    for name, size, me in (("gx", gx, me_x), ("gy", gy, me_y), ("gz", gz, me_z)):
        for d in range(1, size):
            pl.semaphore_signal(
                barrier, inc=1, device_id={name: lax.rem(me + d, size)}, device_id_type=MESH
            )
    local = []
    for r in range(rows):
        for h in range(cuts_a):
            cut = pl.ds(h * part_a, part_a)
            local.append(pltpu.make_async_copy(
                a_ref.at[r, cut], a_all.at[me_x, r, cut], a_recv.at[me_x, r, h]))
    for h in range(cuts_p):
        cut = pl.ds(h * part_p, part_p)
        local.append(pltpu.make_async_copy(
            p_ref.at[cut], p_all.at[me_y, cut], p_recv.at[me_y, h]))
    local.append(pltpu.make_async_copy(m_ref, ma.at[me_x], ma_recv.at[me_x]))
    local.append(pltpu.make_async_copy(m_ref, mp.at[me_y], mp_recv.at[me_y]))
    for copy in local:
        copy.start()
    pl.semaphore_wait(barrier, gx + gy + gz - 3)

    def remote(src, dst, send, recv, where):
        return pltpu.make_async_remote_copy(
            src_ref=src, dst_ref=dst, send_sem=send, recv_sem=recv,
            device_id=where, device_id_type=MESH)

    sends = []
    for d in range(1, gx):
        sends.append(remote(m_ref, ma.at[me_x], ma_send.at[d], ma_recv.at[me_x],
                            {"gx": lax.rem(me_x + d, gx)}))
    for d in range(1, gy):
        sends.append(remote(m_ref, mp.at[me_y], mp_send.at[d], mp_recv.at[me_y],
                            {"gy": lax.rem(me_y + d, gy)}))
    for r in range(rows):
        for h in range(cuts_a):
            cut = pl.ds(h * part_a, part_a)
            for d in range(1, chips):
                sends.append(remote(
                    a_ref.at[r, cut], a_all.at[me_x, r, cut], a_sy.at[d, r, h],
                    a_recv.at[me_x, r, h], {"gx": lax.rem(chip + d, chips) * 2 + core}))
            sends.append(remote(
                a_ref.at[r, cut], a_all.at[me_x, r, cut], a_sp.at[r, h],
                a_recv.at[me_x, r, h], {"gx": partner}))
    for copy in sends:
        copy.start()

    def p_copy(side, src, h, own):
        cut = pl.ds(h * part_p, part_p)
        source = p_ref.at[cut] if own else p_all.at[src, cut]
        step = 1 if side == 0 else -1
        return remote(source, p_all.at[src, cut], p_send.at[side, src, h],
                      p_recv.at[src, h], {"gy": lax.rem(me_y + step + gy, gy)})

    has_next = (me_y + 1 < gy, me_y >= 1)
    for h in range(cuts_p):
        for side in (0, 1):
            @pl.when(has_next[side])
            def _(side=side, h=h):
                p_copy(side, me_y, h, True).start()

    def wait_p(src, h):
        ref = p_all.at[src, pl.ds(h * part_p, part_p)]
        pltpu.make_async_copy(ref, ref, p_recv.at[src, h]).wait()

    def wait_a(g, r, h):
        ref = a_all.at[g, r, pl.ds(h * part_a, part_a)]
        pltpu.make_async_copy(ref, ref, a_recv.at[g, r, h]).wait()

    def split(src):
        pltpu.make_async_copy(mp.at[src], mp.at[src], mp_recv.at[src]).wait()
        copy = pltpu.make_async_copy(mp.at[src], sp.at[src], s_sem)
        copy.start()
        copy.wait()

        def one(k, carry):
            for c in range(COLS_DEV):
                value = jnp.zeros((tile, tile), jnp.float32)
                for s in range(slots_p):
                    code = sp[src, 1, k * slots_p + s]
                    value = value + jnp.where(code == c, p_all[src, k, s], 0.0)
                high = value.astype(jnp.bfloat16)
                low = (value - high.astype(jnp.float32)).astype(jnp.bfloat16)
                p_hi[src * inner + k, :, c * tile:(c + 1) * tile] = high
                p_lo[src * inner + k, :, c * tile:(c + 1) * tile] = low
            return carry

        lax.fori_loop(0, inner, one, 0)

    p_hi[zero_tile] = jnp.zeros_like(p_hi[zero_tile])
    p_lo[zero_tile] = jnp.zeros_like(p_lo[zero_tile])
    for h in range(cuts_p):
        wait_p(me_y, h)
    split(me_y)
    for g in range(gx):
        pltpu.make_async_copy(ma.at[g], ma.at[g], ma_recv.at[g]).wait()
        copy = pltpu.make_async_copy(ma.at[g], sa.at[g], s_sem)
        copy.start()
        copy.wait()

    relays = [(d, r, h) for r in range(rows) for h in range(cuts_a) for d in range(1, chips)]

    def relay_copy(d, r, h):
        src = lax.rem(chip - d + chips, chips) * 2 + core
        cut = pl.ds(h * part_a, part_a)
        ref = a_all.at[src, r, cut]
        return src, remote(ref, ref, a_sf.at[d, r, h], a_recv.at[src, r, h], {"gx": partner})

    def relay(d, r, h):
        src, copy = relay_copy(d, r, h)
        wait_a(src, r, h)
        copy.start()

    steps = [(d, h) for d in range(1, gy) for h in range(cuts_p)]
    done = 0
    for i, (d, h) in enumerate(steps):
        for side in (0, 1):
            src = me_y - d if side == 0 else me_y + d
            there = src >= 0 if side == 0 else src < gy

            @pl.when(there)
            def _(src=src, side=side, h=h):
                wait_p(src, h)

                @pl.when(has_next[side])
                def _():
                    p_copy(side, src, h, False).start()

                if h == cuts_p - 1:
                    split(src)
        goal = (i + 1) * len(relays) // len(steps) if i + 1 < len(steps) else len(relays)
        while done < goal:
            relay(*relays[done])
            done += 1

    def product(q):
        g, r = q // rows, lax.rem(q, rows)
        picks = [sa[g, 0, r * slots + s] for s in range(slots)]
        values = jnp.concatenate([a_all[g, r, s] for s in range(slots)], axis=1)
        high = values.astype(jnp.bfloat16)
        low = (values - high.astype(jnp.float32)).astype(jnp.bfloat16)
        right = jnp.concatenate([p_hi[i] for i in picks], axis=0)
        rest = jnp.concatenate([p_lo[i] for i in picks], axis=0)
        dot = functools.partial(jnp.dot, preferred_element_type=jnp.float32)
        return dot(high, right) + (dot(low, right) + dot(high, rest))

    def await_row(q):
        g, r = q // rows, lax.rem(q, rows)
        mine = jnp.logical_and(g % 2 == core, g // 2 != chip)

        @pl.when(jnp.logical_not(mine))
        def _():
            for h in range(cuts_a):
                wait_a(g, r, h)

    def c_copy(d, i):
        owner = lax.rem(me_z + d, gz)
        return remote(c_send.at[d, i], c_recv.at[d, i], c_ss.at[d, i], c_rs.at[d, i],
                      {"gz": owner})

    for d in range(1, gz):
        def send_row(i, carry, d=d):
            q = lax.rem(me_z + d, gz) * rows_out + i
            await_row(q)
            c_send[d, i] = product(q)
            c_copy(d, i).start()
            return carry

        lax.fori_loop(0, rows_out, send_row, 0)

    def own_row(i, carry):
        q = me_z * rows_out + i
        await_row(q)
        o_ref[pl.ds(pl.multiple_of(i * tile, tile), tile), :] = product(q)
        return carry

    lax.fori_loop(0, rows_out, own_row, 0)

    for d in range(1, gz):
        def add_row(i, carry, d=d):
            pltpu.make_async_copy(c_recv.at[d, i], c_recv.at[d, i], c_rs.at[d, i]).wait()
            at = pl.ds(pl.multiple_of(i * tile, tile), tile)
            o_ref[at, :] = o_ref[at, :] + c_recv[d, i]
            return carry

        lax.fori_loop(0, rows_out, add_row, 0)

    for copy in sends:
        copy.wait_send()
    for d, r, h in relays:
        relay_copy(d, r, h)[1].wait_send()
    for side in (0, 1):
        for d in range(0, gy):
            src = me_y - d if side == 0 else me_y + d
            there = src >= 0 if side == 0 else src < gy

            @pl.when(jnp.logical_and(there, has_next[side]))
            def _(src=src, side=side, d=d):
                for h in range(cuts_p):
                    p_copy(side, src, h, d == 0).wait_send()
    for d in range(1, gz):
        def sent(i, carry, d=d):
            c_copy(d, i).wait_send()
            return carry

        lax.fori_loop(0, rows_out, sent, 0)


def body(gx, gy, gz, a_vals, a_cols, a_count, p_vals, p_cols, p_count):
    rows, slots, tile = a_vals.shape[1], a_vals.shape[3], a_vals.shape[-1]
    inner, slots_p = p_vals.shape[1], p_vals.shape[3]
    alive = jnp.arange(slots, dtype=jnp.int32) < a_count[0, :, 0][:, None]
    picks = jnp.where(alive, a_cols[0, :, 0], gy * inner).reshape(1, -1)
    alive_p = jnp.arange(slots_p, dtype=jnp.int32) < p_count[0, :, 0][:, None]
    codes = jnp.where(alive_p, p_cols[0, :, 0], -1).reshape(1, -1)
    pad = lambda v, at: jnp.pad(v, ((at, 7 - at), (0, 128 - v.shape[1])))
    meta = pad(picks, 0) + pad(codes, 1)
    rows_all = gx * rows
    rows_out = rows_all // gz
    strip = COLS_DEV * tile
    cuts_a = 2 if slots % 2 == 0 else 1
    cuts_p = 2 if inner % 2 == 0 else 1
    dma = pltpu.SemaphoreType.DMA
    any_spec = pl.BlockSpec(memory_space=pl.ANY)
    vmem_spec = pl.BlockSpec(memory_space=pltpu.VMEM)
    return pl.pallas_call(
        functools.partial(kernel, gx, gy, gz),
        out_shape=jax.ShapeDtypeStruct((rows_out * tile, strip), jnp.float32),
        in_specs=[any_spec, any_spec, any_spec],
        out_specs=vmem_spec,
        scratch_shapes=[
            pltpu.VMEM((gx, rows, slots, tile, tile), jnp.float32),
            pltpu.VMEM((gy, inner, slots_p, tile, tile), jnp.float32),
            pltpu.VMEM((gx, 8, 128), jnp.int32),
            pltpu.VMEM((gy, 8, 128), jnp.int32),
            pltpu.SMEM((gx, 8, 128), jnp.int32),
            pltpu.SMEM((gy, 8, 128), jnp.int32),
            pltpu.VMEM((gy * inner + 1, tile, strip), jnp.bfloat16),
            pltpu.VMEM((gy * inner + 1, tile, strip), jnp.bfloat16),
            pltpu.VMEM((gz, rows_out, tile, strip), jnp.float32),
            pltpu.VMEM((gz, rows_out, tile, strip), jnp.float32),
            dma((gx, rows, cuts_a)),
            dma((max(gx // 2, 1), rows, cuts_a)),
            dma((rows, cuts_a)),
            dma((max(gx // 2, 1), rows, cuts_a)),
            dma((gy, cuts_p)),
            dma((2, gy, cuts_p)),
            dma((gx,)),
            dma((gx,)),
            dma((gy,)),
            dma((gy,)),
            dma,
            dma((gz, rows_out)),
            dma((gz, rows_out)),
        ],
        compiler_params=pltpu.CompilerParams(collective_id=0, has_side_effects=True),
    )(a_vals[0, :, 0], p_vals[0, :, 0], meta)


def solution(mesh):
    placed = (
        P("gy", "gx", "gz", None, None, None),
        P("gy", "gx", "gz", None),
        P("gy", "gx", "gz"),
        P("gz", "gy", "gx", None, None, None),
        P("gz", "gy", "gx", None),
        P("gz", "gy", "gx"),
    )
    sizes = (mesh.shape["gx"], mesh.shape["gy"], mesh.shape["gz"])
    return jax.shard_map(
        functools.partial(body, *sizes),
        mesh=mesh, in_specs=placed, out_specs=P(("gy", "gz"), "gx"), check_vma=False,
    )
```

time: 114 us -> 44.7 us (0.39)
  waiting for transfers between devices: 55.1 us -> 0 us
  Pallas kernels: 0 us -> 39.1 us
  blocking collectives: 19 us -> 0 us
  matrix products: 13.1 us -> 0 us
  between operations: 13.1 us -> 0.03 us
  local copies, waits for them, and re-layouts: 9.29 us -> 3.95 us
  other arithmetic: 4.27 us -> 1.34 us
    pallas_call x0 -> x1, Pallas kernels: none -> 39.1 us  [body(): pl.pallas_call(functools.partial(kernel, gx, gy, gz), out_shape=jax.Shape...]
    all_gather x2 -> x0, waiting for transfers between devices: 33.9 us -> none  [the longest x1 25.8 us: body(): tile_part = lax.all_gather(a_masked, 'gx', axis=1, tiled=True)]
    reduce_scatter x1 -> x0, waiting for transfers between devices: 20.5 us -> none  [body(): return lax.psum_scatter(block, 'gz', scatter_dimension=0, tiled=True)]
    all_gather x2 -> x0, blocking collectives: 19 us -> none  [the longest x1 13.7 us: body(): lax.all_gather(weights, 'gy', axis=1, tiled=True)]
    dot_general x2 -> x0, matrix products: 13.1 us -> none  [the longest x1 7.22 us: body(): jnp.einsum('nsij,nspjk->nspik', block_tile_part, chosen, precision=HIGHEST)]
    gather x3 -> x0, local copies, waits for them, and re-layouts: 4.32 us -> none  [the longest x1 3.65 us: body(): chosen = values_all[indices]]
    another operation x2 -> x0, local copies, waits for them, and re-layouts: 3.69 us -> none
    unnamed x1 -> x10, local copies, waits for them, and re-layouts: 1.04 us -> 3.78 us
  transfers between devices with their start and end apart: 3 -> 0, of which waited for: 3 -> 0; matrix products, arithmetic and copies ran while one was open for 8% -> 0% of each run, Pallas kernels for 0% -> 0%
where the time goes in v1:
time: 44.7 us; the launch traced here: 44.5 us
  Pallas kernels  39.1 us (87%)
  local copies, waits for them, and re-layouts  3.95 us (9%)
  other arithmetic  1.34 us (3%)
    pallas_call x1, Pallas kernels, body(): pl.pallas_call(functools.partial(kernel, gx, gy, gz), out_shape=jax.Shape...  39.1 us
    unnamed x10, local copies, waits for them, and re-layouts  3.78 us

profile of v1, /device:TPU:0, one launch (start us, length us, event | category | flops | bytes accessed | tf_op | source)
XLA Modules:
  0.0 44.5 jit_solution(699636493545789637)
XLA Ops:
  0.0 0.0 copy-start
  0.0 0.5 %broadcast.43 = s32[]{:T(128)} broadcast(s32[]{:T(128)} %constant.20), dimensions={} | broadcast | bytes 8 | tf_op args[1]
  0.5 0.2 copy-done
  0.7 0.7 %reduce.3 = s32[2,6]{1,0:T(2,128)S(1)} reduce(s32[1,2,1,6]{3,2,1,0:T(1,128)S(1)} %copy-done, s32[]{:T(128)} %broadcast.43), dimensions={0,2}, to_apply=%param.7.reduce_sub_computation.3 | reduce | bytes 100 | tf_op args[1]
  1.3 0.0 copy-start.1
  1.4 0.1 squeeze.14
  1.4 0.6 %copy-done.1 = s32[1,2,1]{1,2,0:T(1,128)S(1)} copy-done((s32[1,2,1]{1,2,0:T(1,128)S(1)}, s32[1,2,1]{1,2,0:T(1,128)}, u32[]{:S(2)}) %copy-start.1) | copy-done | bytes 32
  2.0 0.1 iota_compare_fusion
  2.1 0.1 lt.44
  2.2 0.0 copy-start.2
  2.2 0.0 copy-start.3
  2.2 0.6 %copy-done.2 = s32[1,4,1]{1,2,0:T(1,128)S(1)} copy-done((s32[1,4,1]{1,2,0:T(1,128)S(1)}, s32[1,4,1]{1,2,0:T(1,128)}, u32[]{:S(2)}) %copy-start.2) | copy-done | bytes 40
  2.8 0.0 copy-done.3
  2.8 0.6 %pad_add_fusion.m_ref = s32[8,128]{1,0:T(8,128)} fusion(s32[1,4]{1,0:T(1,128)S(1)} %bitcast_select_fusion, s32[1,12]{1,0:T(1,128)S(1)} %broadcast_select_fusion), kind=kLoop, calls=%fused_computation | loop fusion | flops 1024 | bytes 4160 | tf_op jit(solution)/shard_map/add | solution.py:250
  3.4 39.1 %shard_map.64 = f32[512,256]{1,0:T(8,128)} custom-call(f32[2,6,128,128]{3,2,1,0:T(8,128)} %bitcast.7, f32[4,1,128,128]{3,2,1,0:T(8,128)} %bitcast.8, s32[8,128]{1,0:T(8,128)} %pad_add_fusion.m_ref), custom_call_target="tpu_custom_call" | custom-call | tf_op jit(solution)/shard_map/pallas_call | solution.py:259
  42.6 1.9 %copy.8 = f32[512,256]{1,0:T(8,128)} copy(f32[512,256]{1,0:T(8,128)} %shard_map.64) | data formatting | bytes 1048576
  (2 shorter events, 0.0 us)
Async XLA Ops:
  0.0 0.7 %copy-start = (s32[1,2,1,6]{3,2,1,0:T(1,128)S(1)}, s32[1,2,1,6]{3,2,1,0:T(1,128)}, u32[]{:S(2)}) copy-start(s32[1,2,1,6]{3,2,1,0:T(1,128)} %param.7) | copy-start | bytes 148
  1.3 0.7 %copy-start.1 = (s32[1,2,1]{1,2,0:T(1,128)S(1)}, s32[1,2,1]{1,2,0:T(1,128)}, u32[]{:S(2)}) copy-start(s32[1,2,1]{1,2,0:T(1,128)} %param.8) | copy-start | bytes 28
  2.2 0.7 %copy-start.2 = (s32[1,4,1]{1,2,0:T(1,128)S(1)}, s32[1,4,1]{1,2,0:T(1,128)}, u32[]{:S(2)}) copy-start(s32[1,4,1]{1,2,0:T(1,128)} %param.11) | copy-start | bytes 52
  2.2 0.7 %copy-start.3 = (s32[1,4,1,1]{1,3,2,0:T(1,128)S(1)}, s32[1,4,1,1]{1,3,2,0:T(1,128)}, u32[]{:S(2)}) copy-start(s32[1,4,1,1]{1,3,2,0:T(1,128)} %param.10) | copy-start | bytes 52

commit v2 on v1

v2 whole, which is shorter than its diff:
```python
import functools

import jax
import jax.numpy as jnp
from jax import lax
from jax.experimental import pallas as pl
from jax.experimental.pallas import tpu as pltpu
from jax.sharding import PartitionSpec as P

COLS_DEV = 2
MESH = pl.DeviceIdType.MESH


def kernel(
    gx, gy, gz, slots_p,
    a_ref, p_ref, ac_ref, an_ref, pc_ref, pn_ref, o_ref,
    a_all, p_own, p_all, ma, mp, sa, sp, p_mul, c_send, c_recv,
    a_recv, a_sy, a_sp, a_sf, p_load, p_recv, p_send,
    ma_recv, ma_send, mp_recv, mp_send, s_sem, c_rs, c_ss,
):
    rows, slots, tile = a_ref.shape[0], a_ref.shape[1], a_ref.shape[2]
    tiles_p = p_ref.shape[0]
    inner = tiles_p // slots_p
    pairs = p_all.shape[2]
    rows_all = gx * rows
    rows_out = rows_all // gz
    zero_tile = gy * inner
    half = tile // 2
    cuts_a = a_recv.shape[2]
    part_a = slots // cuts_a
    me_x, me_y, me_z = lax.axis_index("gx"), lax.axis_index("gy"), lax.axis_index("gz")
    chips = gx // 2
    chip, core = me_x // 2, me_x % 2
    partner = chip * 2 + (1 - core)

    barrier = pltpu.get_barrier_semaphore()
    for name, size, me in (("gx", gx, me_x), ("gy", gy, me_y), ("gz", gz, me_z)):
        for d in range(1, size):
            pl.semaphore_signal(
                barrier, inc=1, device_id={name: lax.rem(me + d, size)}, device_id_type=MESH
            )
    load = pltpu.make_async_copy(p_ref, p_own, p_load)
    load.start()
    for r in range(rows):
        for h in range(cuts_a):
            cut = pl.ds(h * part_a, part_a)
            pltpu.make_async_copy(
                a_ref.at[r, cut], a_all.at[me_x, r, cut], a_recv.at[me_x, r, h]).start()

    line = lax.broadcasted_iota(jnp.int32, (8, 128), 0)
    lane = lax.broadcasted_iota(jnp.int32, (8, 128), 1)
    meta = jnp.zeros((8, 128), jnp.int32)
    for r in range(rows):
        for s in range(slots):
            pick = jnp.where(s < an_ref[r], ac_ref[0, r, 0, s], zero_tile)
            meta = jnp.where((line == 0) & (lane == r * slots + s), pick, meta)
    for t in range(tiles_p):
        code = jnp.where(t % slots_p < pn_ref[t // slots_p], pc_ref[t], -1)
        meta = jnp.where((line == 1) & (lane == t), code, meta)
    ma[me_x] = meta
    mp[me_y] = meta
    p_mul[0, zero_tile] = jnp.zeros_like(p_mul[0, zero_tile])
    p_mul[1, zero_tile] = jnp.zeros_like(p_mul[1, zero_tile])

    left = lax.broadcasted_iota(jnp.int32, (tile, tile), 1) < half
    load.wait()
    for j in range(pairs):
        one, two = p_own[2 * j], p_own[min(2 * j + 1, tiles_p - 1)]
        p_all[me_y, 0, j] = jnp.where(left, one, pltpu.roll(two, half, 1))
        p_all[me_y, 1, j] = jnp.where(left, pltpu.roll(one, half, 1), two)

    pl.semaphore_wait(barrier, gx + gy + gz - 3)

    def remote(src, dst, send, recv, where):
        return pltpu.make_async_remote_copy(
            src_ref=src, dst_ref=dst, send_sem=send, recv_sem=recv,
            device_id=where, device_id_type=MESH)

    sends = []
    for d in range(1, gx):
        sends.append(remote(ma.at[me_x], ma.at[me_x], ma_send.at[d], ma_recv.at[me_x],
                            {"gx": lax.rem(me_x + d, gx)}))
    for d in range(1, gy):
        sends.append(remote(mp.at[me_y], mp.at[me_y], mp_send.at[d], mp_recv.at[me_y],
                            {"gy": lax.rem(me_y + d, gy)}))
    for r in range(rows):
        for h in range(cuts_a):
            cut = pl.ds(h * part_a, part_a)
            for d in range(1, chips):
                sends.append(remote(
                    a_ref.at[r, cut], a_all.at[me_x, r, cut], a_sy.at[d, r, h],
                    a_recv.at[me_x, r, h], {"gx": lax.rem(chip + d, chips) * 2 + core}))
            sends.append(remote(
                a_ref.at[r, cut], a_all.at[me_x, r, cut], a_sp.at[r, h],
                a_recv.at[me_x, r, h], {"gx": partner}))
    for copy in sends:
        copy.start()

    def p_copy(side, src, h, j):
        ref = p_all.at[src, h, j]
        step = 1 if side == 0 else -1
        return remote(ref, ref, p_send.at[side, src, h, j], p_recv.at[src, h, j],
                      {"gy": lax.rem(me_y + step + gy, gy)})

    has_next = (me_y + 1 < gy, me_y >= 1)

    def send_own(h):
        for j in range(pairs):
            for side in (0, 1):
                @pl.when(has_next[side])
                def _(side=side, j=j):
                    p_copy(side, me_y, h, j).start()

    send_own(0)

    def wait_a(g, r, h):
        ref = a_all.at[g, r, pl.ds(h * part_a, part_a)]
        pltpu.make_async_copy(ref, ref, a_recv.at[g, r, h]).wait()

    for d in range(1, gx):
        g = lax.rem(me_x + d, gx)
        pltpu.make_async_copy(ma.at[g], ma.at[g], ma_recv.at[g]).wait()
    for d in range(1, gy):
        g = lax.rem(me_y + d, gy)
        pltpu.make_async_copy(mp.at[g], mp.at[g], mp_recv.at[g]).wait()
    moves = [pltpu.make_async_copy(ma, sa, s_sem.at[0]), pltpu.make_async_copy(mp, sp, s_sem.at[1])]
    for copy in moves:
        copy.start()
    for copy in moves:
        copy.wait()

    side_of_lane = lax.broadcasted_iota(jnp.int32, (tile, tile), 1) // half

    def split(src, h):
        def one(k, carry):
            value = jnp.zeros((tile, tile), jnp.float32)
            for s in range(slots_p):
                t = k * slots_p + s
                code = sp[src, 1, t]
                packed = p_all[src, h, t // 2]
                turned = pltpu.roll(packed, half, 1)
                placed = jnp.where(code == t % 2, packed, turned)
                value = value + jnp.where(side_of_lane == code, placed, 0.0)
            high = value.astype(jnp.bfloat16)
            low = (value - high.astype(jnp.float32)).astype(jnp.bfloat16)
            p_mul[h, src * inner + k, :, :tile] = high
            p_mul[h, src * inner + k, :, tile:] = low
            return carry

        lax.fori_loop(0, inner, one, 0)

    def relay_copy(d, r, h):
        src = lax.rem(chip - d + chips, chips) * 2 + core
        ref = a_all.at[src, r, pl.ds(h * part_a, part_a)]
        return src, remote(ref, ref, a_sf.at[d, r, h], a_recv.at[src, r, h], {"gx": partner})

    def relay(d, r, h):
        src, copy = relay_copy(d, r, h)
        wait_a(src, r, h)
        copy.start()

    def source(side, d):
        src = me_y - d if side == 0 else me_y + d
        return src, src >= 0 if side == 0 else src < gy

    def gather_half(h, relays):
        done = 0
        for d in range(1, gy):
            for side in (0, 1):
                src, there = source(side, d)

                @pl.when(there)
                def _(src=src, side=side):
                    for j in range(pairs):
                        ref = p_all.at[src, h, j]
                        pltpu.make_async_copy(ref, ref, p_recv.at[src, h, j]).wait()

                        @pl.when(has_next[side])
                        def _(j=j):
                            p_copy(side, src, h, j).start()

                    split(src, h)
            if h == 0 and d == max(gy - 2, 1):
                send_own(1)
            goal = max(0, d - 1) * len(relays) // (gy - 1)
            while done < goal:
                relay(*relays[done])
                done += 1
        while done < len(relays):
            relay(*relays[done])
            done += 1

    relays = [(d, r, h) for r in range(rows) for h in range(cuts_a) for d in range(1, chips)]

    def product(q, h):
        g, r = q // rows, lax.rem(q, rows)
        picks = [sa[g, 0, r * slots + s] for s in range(slots)]
        values = jnp.concatenate([a_all[g, r, s] for s in range(slots)], axis=1)
        high = values.astype(jnp.bfloat16)
        low = (values - high.astype(jnp.float32)).astype(jnp.bfloat16)
        right = jnp.concatenate([p_mul[h, i] for i in picks], axis=0)
        out = jnp.dot(jnp.concatenate([high, low], axis=0), right,
                      preferred_element_type=jnp.float32)
        return out[:tile, :tile] + (out[:tile, tile:] + out[tile:, :tile] + out[tile:, tile:])

    def await_row(q):
        g, r = q // rows, lax.rem(q, rows)
        mine = jnp.logical_and(g % 2 == core, g // 2 != chip)

        @pl.when(jnp.logical_not(mine))
        def _():
            for h in range(cuts_a):
                wait_a(g, r, h)

    def c_copy(d, i, h):
        return remote(c_send.at[d, i, h], c_recv.at[d, i, h], c_ss.at[d, i, h],
                      c_rs.at[d, i, h], {"gz": lax.rem(me_z + d, gz)})

    def send_rows(lines, halves, first):
        for d in range(1, gz):
            def send_row(n, carry, d=d):
                i = lines[0] + n * (lines[1] - lines[0] if len(lines) > 1 else 1)
                q = lax.rem(me_z + d, gz) * rows_out + i
                if first:
                    await_row(q)
                for h in halves:
                    c_send[d, i, h] = product(q, h)
                    c_copy(d, i, h).start()
                return carry

            lax.fori_loop(0, len(lines), send_row, 0)

    early = list(range(0, rows_out, rows))
    split(me_y, 0)
    gather_half(0, [x for x in relays if x[1] == 0])
    send_rows(early, (0,), True)
    split(me_y, 1)
    gather_half(1, [x for x in relays if x[1] > 0])
    send_rows(early, (1,), False)
    for r in range(1, rows):
        late = list(range(r, rows_out, rows))
        if late:
            send_rows(late, (0, 1), True)

    def own_row(i, carry):
        q = me_z * rows_out + i
        await_row(q)
        for h in (0, 1):
            c_send[0, i, h] = product(q, h)
        return carry

    lax.fori_loop(0, rows_out, own_row, 0)

    def finish(i):
        halves = []
        for h in (0, 1):
            value = c_send[0, i, h]
            for d in range(1, gz):
                ref = c_recv.at[d, i, h]
                pltpu.make_async_copy(ref, ref, c_rs.at[d, i, h]).wait()
                value = value + c_recv[d, i, h]
            halves.append(value)
        one, two = halves
        at = pl.ds(i * tile, tile)
        o_ref[at, :tile] = jnp.where(left, one, pltpu.roll(two, half, 1))
        o_ref[at, tile:] = jnp.where(left, pltpu.roll(one, half, 1), two)

    for r in range(rows):
        for i in range(r, rows_out, rows):
            finish(i)

    for copy in sends:
        copy.wait_send()
    for d, r, h in relays:
        relay_copy(d, r, h)[1].wait_send()
    for side in (0, 1):
        for d in range(0, gy):
            src, there = source(side, d)

            @pl.when(jnp.logical_and(there, has_next[side]))
            def _(src=src, side=side):
                for h in (0, 1):
                    for j in range(pairs):
                        p_copy(side, src, h, j).wait_send()
    for d in range(1, gz):
        for i in range(rows_out):
            for h in (0, 1):
                c_copy(d, i, h).wait_send()


def body(gx, gy, gz, a_vals, a_cols, a_count, p_vals, p_cols, p_count):
    rows, slots, tile = a_vals.shape[1], a_vals.shape[3], a_vals.shape[-1]
    inner, slots_p = p_vals.shape[1], p_vals.shape[3]
    tiles_p = inner * slots_p
    pairs = (tiles_p + 1) // 2
    rows_out = gx * rows // gz
    cuts_a = 2 if slots % 2 == 0 else 1
    dma = pltpu.SemaphoreType.DMA
    any_spec = pl.BlockSpec(memory_space=pl.ANY)
    smem_spec = pl.BlockSpec(memory_space=pltpu.SMEM)
    return pl.pallas_call(
        functools.partial(kernel, gx, gy, gz, slots_p),
        out_shape=jax.ShapeDtypeStruct((rows_out * tile, COLS_DEV * tile), jnp.float32),
        in_specs=[any_spec] * 2 + [smem_spec] * 4,
        out_specs=pl.BlockSpec(memory_space=pltpu.VMEM),
        scratch_shapes=[
            pltpu.VMEM((gx, rows, slots, tile, tile), jnp.float32),
            pltpu.VMEM((tiles_p, tile, tile), jnp.float32),
            pltpu.VMEM((gy, 2, pairs, tile, tile), jnp.float32),
            pltpu.VMEM((gx, 8, 128), jnp.int32),
            pltpu.VMEM((gy, 8, 128), jnp.int32),
            pltpu.SMEM((gx, 8, 128), jnp.int32),
            pltpu.SMEM((gy, 8, 128), jnp.int32),
            pltpu.VMEM((2, gy * inner + 1, tile, 2 * tile), jnp.bfloat16),
            pltpu.VMEM((gz, rows_out, 2, tile, tile), jnp.float32),
            pltpu.VMEM((gz, rows_out, 2, tile, tile), jnp.float32),
            dma((gx, rows, cuts_a)),
            dma((max(gx // 2, 1), rows, cuts_a)),
            dma((rows, cuts_a)),
            dma((max(gx // 2, 1), rows, cuts_a)),
            dma,
            dma((gy, 2, pairs)),
            dma((2, gy, 2, pairs)),
            dma((gx,)),
            dma((gx,)),
            dma((gy,)),
            dma((gy,)),
            dma((2,)),
            dma((gz, rows_out, 2)),
            dma((gz, rows_out, 2)),
        ],
        compiler_params=pltpu.CompilerParams(collective_id=0, has_side_effects=True),
    )(
        a_vals[0, :, 0], p_vals.reshape(tiles_p, tile, tile),
        a_cols, a_count.reshape(-1), p_cols.reshape(-1), p_count.reshape(-1),
    )


def solution(mesh):
    placed = (
        P("gy", "gx", "gz", None, None, None),
        P("gy", "gx", "gz", None),
        P("gy", "gx", "gz"),
        P("gz", "gy", "gx", None, None, None),
        P("gz", "gy", "gx", None),
        P("gz", "gy", "gx"),
    )
    sizes = (mesh.shape["gx"], mesh.shape["gy"], mesh.shape["gz"])
    return jax.shard_map(
        functools.partial(body, *sizes),
        mesh=mesh, in_specs=placed, out_specs=P(("gy", "gz"), "gx"), check_vma=False,
    )
```

time: 44.7 us -> 40.3 us (0.902)
  local copies, waits for them, and re-layouts: 3.95 us -> 1.87 us
  other arithmetic: 1.34 us -> 0 us
  Pallas kernels: 39.1 us -> 38.2 us
    unnamed x10 -> x1, local copies, waits for them, and re-layouts: 3.78 us -> 1.87 us
    pallas_call x1, Pallas kernels: 39.1 us -> 38.2 us  [body(): pl.pallas_call(functools.partial(kernel, gx, gy, gz, slots_p), out_shape=...]
    unnamed x1 -> x0, other arithmetic: 0.66 us -> none
    add x1 -> x0, other arithmetic: 0.6 us -> none  [body(): meta = pad(picks, 0) + pad(codes, 1)]
where the time goes in v2:
time: 40.3 us; the launch traced here: 40.1 us
  Pallas kernels  38.2 us (95%)
  local copies, waits for them, and re-layouts  1.87 us (5%)
    pallas_call x1, Pallas kernels, body(): pl.pallas_call(functools.partial(kernel, gx, gy, gz, slots_p), out_shape=...  38.2 us
    unnamed x1, local copies, waits for them, and re-layouts  1.87 us

profile of v2, /device:TPU:0, one launch (start us, length us, event | category | flops | bytes accessed | tf_op | source)
XLA Modules:
  0.0 40.1 jit_solution(4808773853659401375)
XLA Ops:
  0.0 38.2 %shard_map.64 = f32[512,256]{1,0:T(8,128)} custom-call(f32[2,6,128,128]{3,2,1,0:T(8,128)} %bitcast.5, f32[4,128,128]{2,1,0:T(8,128)} %bitcast.6, s32[1,2,1,6]{3,2,1,0:T(1,128)} %ac_ref.1, s32[2]{0:T(128)} %bitcast.7, s32[4]{0:T(128)} %bitcast.8, s32[4]{0:T(128)} %bitcast.9), custom_call_target="tpu_custom_call" | custom-call | tf_op jit(solution)/shard_map/pallas_call | solution.py:301
  38.2 1.9 %copy.8 = f32[512,256]{1,0:T(8,128)} copy(f32[512,256]{1,0:T(8,128)} %shard_map.64) | data formatting | bytes 1048576

commit v3 on v2

--- a/solution.py
+++ b/solution.py
@@ -13,8 +13,8 @@
 
 def kernel(
     gx, gy, gz, slots_p,
-    a_ref, p_ref, ac_ref, an_ref, pc_ref, pn_ref, o_ref,
-    a_all, p_own, p_all, ma, mp, sa, sp, p_mul, c_send, c_recv,
+    a_ref, p_ref, ac_hbm, an_hbm, pc_hbm, pn_hbm, o_ref,
+    ac_ref, an_ref, pc_ref, pn_ref, i_load, a_all, p_own, p_all, ma, mp, sa, sp, p_mul, c_send, c_recv,
     a_recv, a_sy, a_sp, a_sf, p_load, p_recv, p_send,
     ma_recv, ma_send, mp_recv, mp_send, s_sem, c_rs, c_ss,
 ):
@@ -41,12 +41,67 @@
             )
     load = pltpu.make_async_copy(p_ref, p_own, p_load)
     load.start()
+    small = [
+        pltpu.make_async_copy(src, dst, i_load.at[n])
+        for n, (src, dst) in enumerate((
+            (ac_hbm, ac_ref), (an_hbm, an_ref), (pc_hbm, pc_ref), (pn_hbm, pn_ref)))
+    ]
+    for copy in small:
+        copy.start()
     for r in range(rows):
         for h in range(cuts_a):
             cut = pl.ds(h * part_a, part_a)
             pltpu.make_async_copy(
                 a_ref.at[r, cut], a_all.at[me_x, r, cut], a_recv.at[me_x, r, h]).start()
 
+    pl.semaphore_wait(barrier, gx + gy + gz - 3)
+
+    def remote(src, dst, send, recv, where):
+        return pltpu.make_async_remote_copy(
+            src_ref=src, dst_ref=dst, send_sem=send, recv_sem=recv,
+            device_id=where, device_id_type=MESH)
+
+    sends = []
+    for r in range(rows):
+        for h in range(cuts_a):
+            cut = pl.ds(h * part_a, part_a)
+            for d in range(1, chips):
+                sends.append(remote(
+                    a_ref.at[r, cut], a_all.at[me_x, r, cut], a_sy.at[d, r, h],
+                    a_recv.at[me_x, r, h], {"gx": lax.rem(chip + d, chips) * 2 + core}))
+            sends.append(remote(
+                a_ref.at[r, cut], a_all.at[me_x, r, cut], a_sp.at[r, h],
+                a_recv.at[me_x, r, h], {"gx": partner}))
+    for copy in sends:
+        copy.start()
+    large = len(sends)
+
+    left = lax.broadcasted_iota(jnp.int32, (tile, tile), 1) < half
+    load.wait()
+    for j in range(pairs):
+        one, two = p_own[2 * j], p_own[min(2 * j + 1, tiles_p - 1)]
+        p_all[me_y, 0, j] = jnp.where(left, one, pltpu.roll(two, half, 1))
+        p_all[me_y, 1, j] = jnp.where(left, pltpu.roll(one, half, 1), two)
+
+    def p_copy(side, src, h, j):
+        ref = p_all.at[src, h, j]
+        step = 1 if side == 0 else -1
+        return remote(ref, ref, p_send.at[side, src, h, j], p_recv.at[src, h, j],
+                      {"gy": lax.rem(me_y + step + gy, gy)})
+
+    has_next = (me_y + 1 < gy, me_y >= 1)
+
+    def send_own(h):
+        for j in range(pairs):
+            for side in (0, 1):
+                @pl.when(has_next[side])
+                def _(side=side, j=j):
+                    p_copy(side, me_y, h, j).start()
+
+    send_own(0)
+
+    for copy in small:
+        copy.wait()
     line = lax.broadcasted_iota(jnp.int32, (8, 128), 0)
     lane = lax.broadcasted_iota(jnp.int32, (8, 128), 1)
     meta = jnp.zeros((8, 128), jnp.int32)
@@ -62,72 +117,31 @@
     p_mul[0, zero_tile] = jnp.zeros_like(p_mul[0, zero_tile])
     p_mul[1, zero_tile] = jnp.zeros_like(p_mul[1, zero_tile])
 
-    left = lax.broadcasted_iota(jnp.int32, (tile, tile), 1) < half
-    load.wait()
-    for j in range(pairs):
-        one, two = p_own[2 * j], p_own[min(2 * j + 1, tiles_p - 1)]
-        p_all[me_y, 0, j] = jnp.where(left, one, pltpu.roll(two, half, 1))
-        p_all[me_y, 1, j] = jnp.where(left, pltpu.roll(one, half, 1), two)
-
-    pl.semaphore_wait(barrier, gx + gy + gz - 3)
-
-    def remote(src, dst, send, recv, where):
-        return pltpu.make_async_remote_copy(
-            src_ref=src, dst_ref=dst, send_sem=send, recv_sem=recv,
-            device_id=where, device_id_type=MESH)
-
-    sends = []
     for d in range(1, gx):
         sends.append(remote(ma.at[me_x], ma.at[me_x], ma_send.at[d], ma_recv.at[me_x],
                             {"gx": lax.rem(me_x + d, gx)}))
     for d in range(1, gy):
         sends.append(remote(mp.at[me_y], mp.at[me_y], mp_send.at[d], mp_recv.at[me_y],
                             {"gy": lax.rem(me_y + d, gy)}))
-    for r in range(rows):
-        for h in range(cuts_a):
-            cut = pl.ds(h * part_a, part_a)
-            for d in range(1, chips):
-                sends.append(remote(
-                    a_ref.at[r, cut], a_all.at[me_x, r, cut], a_sy.at[d, r, h],
-                    a_recv.at[me_x, r, h], {"gx": lax.rem(chip + d, chips) * 2 + core}))
-            sends.append(remote(
-                a_ref.at[r, cut], a_all.at[me_x, r, cut], a_sp.at[r, h],
-                a_recv.at[me_x, r, h], {"gx": partner}))
-    for copy in sends:
+    for copy in sends[large:]:
         copy.start()
-
-    def p_copy(side, src, h, j):
-        ref = p_all.at[src, h, j]
-        step = 1 if side == 0 else -1
-        return remote(ref, ref, p_send.at[side, src, h, j], p_recv.at[src, h, j],
-                      {"gy": lax.rem(me_y + step + gy, gy)})
-
-    has_next = (me_y + 1 < gy, me_y >= 1)
-
-    def send_own(h):
-        for j in range(pairs):
-            for side in (0, 1):
-                @pl.when(has_next[side])
-                def _(side=side, j=j):
-                    p_copy(side, me_y, h, j).start()
-
-    send_own(0)
 
     def wait_a(g, r, h):
         ref = a_all.at[g, r, pl.ds(h * part_a, part_a)]
         pltpu.make_async_copy(ref, ref, a_recv.at[g, r, h]).wait()
 
-    for d in range(1, gx):
-        g = lax.rem(me_x + d, gx)
-        pltpu.make_async_copy(ma.at[g], ma.at[g], ma_recv.at[g]).wait()
-    for d in range(1, gy):
-        g = lax.rem(me_y + d, gy)
-        pltpu.make_async_copy(mp.at[g], mp.at[g], mp_recv.at[g]).wait()
-    moves = [pltpu.make_async_copy(ma, sa, s_sem.at[0]), pltpu.make_async_copy(mp, sp, s_sem.at[1])]
-    for copy in moves:
-        copy.start()
-    for copy in moves:
-        copy.wait()
+    def indices():
+        for d in range(1, gx):
+            g = lax.rem(me_x + d, gx)
+            pltpu.make_async_copy(ma.at[g], ma.at[g], ma_recv.at[g]).wait()
+        for d in range(1, gy):
+            g = lax.rem(me_y + d, gy)
+            pltpu.make_async_copy(mp.at[g], mp.at[g], mp_recv.at[g]).wait()
+        moves = [pltpu.make_async_copy(ma, sa, s_sem.at[0]), pltpu.make_async_copy(mp, sp, s_sem.at[1])]
+        for copy in moves:
+            copy.start()
+        for copy in moves:
+            copy.wait()
 
     side_of_lane = lax.broadcasted_iota(jnp.int32, (tile, tile), 1) // half
 
@@ -179,7 +193,17 @@
                         def _(j=j):
                             p_copy(side, src, h, j).start()
 
+            if d == 1:
+                if h == 0:
+                    indices()
+                split(me_y, h)
+            for side in (0, 1):
+                src, there = source(side, d)
+
+                @pl.when(there)
+                def _(src=src):
                     split(src, h)
+
             if h == 0 and d == max(gy - 2, 1):
                 send_own(1)
             goal = max(0, d - 1) * len(relays) // (gy - 1)
@@ -231,10 +255,8 @@
             lax.fori_loop(0, len(lines), send_row, 0)
 
     early = list(range(0, rows_out, rows))
-    split(me_y, 0)
     gather_half(0, [x for x in relays if x[1] == 0])
     send_rows(early, (0,), True)
-    split(me_y, 1)
     gather_half(1, [x for x in relays if x[1] > 0])
     send_rows(early, (1,), False)
     for r in range(1, rows):
@@ -297,13 +319,17 @@
     cuts_a = 2 if slots % 2 == 0 else 1
     dma = pltpu.SemaphoreType.DMA
     any_spec = pl.BlockSpec(memory_space=pl.ANY)
-    smem_spec = pl.BlockSpec(memory_space=pltpu.SMEM)
     return pl.pallas_call(
         functools.partial(kernel, gx, gy, gz, slots_p),
         out_shape=jax.ShapeDtypeStruct((rows_out * tile, COLS_DEV * tile), jnp.float32),
-        in_specs=[any_spec] * 2 + [smem_spec] * 4,
+        in_specs=[any_spec] * 6,
         out_specs=pl.BlockSpec(memory_space=pltpu.VMEM),
         scratch_shapes=[
+            pltpu.SMEM(a_cols.shape, jnp.int32),
+            pltpu.SMEM((rows,), jnp.int32),
+            pltpu.SMEM((tiles_p,), jnp.int32),
+            pltpu.SMEM((inner,), jnp.int32),
+            dma((4,)),
             pltpu.VMEM((gx, rows, slots, tile, tile), jnp.float32),
             pltpu.VMEM((tiles_p, tile, tile), jnp.float32),
             pltpu.VMEM((gy, 2, pairs, tile, tile), jnp.float32),

time: 40.3 us -> 54.1 us (1.34)
  Pallas kernels: 38.2 us -> 52.1 us
    pallas_call x1, Pallas kernels: 38.2 us -> 52.1 us  [body(): pl.pallas_call(functools.partial(kernel, gx, gy, gz, slots_p), out_shape=...]
where the time goes in v3:
time: 54.1 us; the launch traced here: 54 us
  Pallas kernels  52.1 us (96%)
  local copies, waits for them, and re-layouts  1.87 us (3%)
    pallas_call x1, Pallas kernels, body(): pl.pallas_call(functools.partial(kernel, gx, gy, gz, slots_p), out_shape=...  52.1 us
    unnamed x1, local copies, waits for them, and re-layouts  1.87 us

profile of v3, /device:TPU:0, one launch (start us, length us, event | category | flops | bytes accessed | tf_op | source)
XLA Modules:
  0.0 54.0 jit_solution(13597849114571213281)
XLA Ops:
  0.0 52.1 %shard_map.64 = f32[512,256]{1,0:T(8,128)} custom-call(f32[2,6,128,128]{3,2,1,0:T(8,128)} %bitcast.5, f32[4,128,128]{2,1,0:T(8,128)} %bitcast.6, s32[1,2,1,6]{3,2,1,0:T(1,128)} %ac_hbm.1, s32[2]{0:T(128)} %bitcast.7, s32[4]{0:T(128)} %bitcast.8, s32[4]{0:T(128)} %bitcast.9), custom_call_target="tpu_custom_call" | custom-call | tf_op jit(solution)/shard_map/pallas_call | solution.py:322
  52.1 1.9 %copy.8 = f32[512,256]{1,0:T(8,128)} copy(f32[512,256]{1,0:T(8,128)} %shard_map.64) | data formatting | bytes 1048576

commit v4 on v3

--- a/solution.py
+++ b/solution.py
@@ -72,9 +72,10 @@
             sends.append(remote(
                 a_ref.at[r, cut], a_all.at[me_x, r, cut], a_sp.at[r, h],
                 a_recv.at[me_x, r, h], {"gx": partner}))
-    for copy in sends:
-        copy.start()
     large = len(sends)
+    first = large // rows
+    for copy in sends[:first]:
+        copy.start()
 
     left = lax.broadcasted_iota(jnp.int32, (tile, tile), 1) < half
     load.wait()
@@ -123,25 +124,20 @@
     for d in range(1, gy):
         sends.append(remote(mp.at[me_y], mp.at[me_y], mp_send.at[d], mp_recv.at[me_y],
                             {"gy": lax.rem(me_y + d, gy)}))
-    for copy in sends[large:]:
+    for copy in sends[large:] + sends[first:large]:
         copy.start()
 
     def wait_a(g, r, h):
         ref = a_all.at[g, r, pl.ds(h * part_a, part_a)]
         pltpu.make_async_copy(ref, ref, a_recv.at[g, r, h]).wait()
 
-    def indices():
-        for d in range(1, gx):
-            g = lax.rem(me_x + d, gx)
-            pltpu.make_async_copy(ma.at[g], ma.at[g], ma_recv.at[g]).wait()
-        for d in range(1, gy):
-            g = lax.rem(me_y + d, gy)
-            pltpu.make_async_copy(mp.at[g], mp.at[g], mp_recv.at[g]).wait()
-        moves = [pltpu.make_async_copy(ma, sa, s_sem.at[0]), pltpu.make_async_copy(mp, sp, s_sem.at[1])]
-        for copy in moves:
-            copy.start()
-        for copy in moves:
-            copy.wait()
+    def indices(size, me, held, scalars, arrived, n):
+        for d in range(1, size):
+            g = lax.rem(me + d, size)
+            pltpu.make_async_copy(held.at[g], held.at[g], arrived.at[g]).wait()
+        copy = pltpu.make_async_copy(held, scalars, s_sem.at[n])
+        copy.start()
+        copy.wait()
 
     side_of_lane = lax.broadcasted_iota(jnp.int32, (tile, tile), 1) // half
 
@@ -195,7 +191,7 @@
 
             if d == 1:
                 if h == 0:
-                    indices()
+                    indices(gy, me_y, mp, sp, mp_recv, 1)
                 split(me_y, h)
             for side in (0, 1):
                 src, there = source(side, d)
@@ -256,6 +252,7 @@
 
     early = list(range(0, rows_out, rows))
     gather_half(0, [x for x in relays if x[1] == 0])
+    indices(gx, me_x, ma, sa, ma_recv, 0)
     send_rows(early, (0,), True)
     gather_half(1, [x for x in relays if x[1] > 0])
     send_rows(early, (1,), False)

time: 54.1 us -> 40.6 us (0.75)
  Pallas kernels: 52.1 us -> 38.6 us
    pallas_call x1, Pallas kernels: 52.1 us -> 38.6 us  [body(): pl.pallas_call(functools.partial(kernel, gx, gy, gz, slots_p), out_shape=...]
where the time goes in v4:
time: 40.6 us; the launch traced here: 40.5 us
  Pallas kernels  38.6 us (95%)
  local copies, waits for them, and re-layouts  1.87 us (5%)
    pallas_call x1, Pallas kernels, body(): pl.pallas_call(functools.partial(kernel, gx, gy, gz, slots_p), out_shape=...  38.6 us
    unnamed x1, local copies, waits for them, and re-layouts  1.87 us

profile of v4, /device:TPU:0, one launch (start us, length us, event | category | flops | bytes accessed | tf_op | source)
XLA Modules:
  0.0 40.5 jit_solution(9094446147315526571)
XLA Ops:
  0.0 38.6 %shard_map.64 = f32[512,256]{1,0:T(8,128)} custom-call(f32[2,6,128,128]{3,2,1,0:T(8,128)} %bitcast.5, f32[4,128,128]{2,1,0:T(8,128)} %bitcast.6, s32[1,2,1,6]{3,2,1,0:T(1,128)} %ac_hbm.1, s32[2]{0:T(128)} %bitcast.7, s32[4]{0:T(128)} %bitcast.8, s32[4]{0:T(128)} %bitcast.9), custom_call_target="tpu_custom_call" | custom-call | tf_op jit(solution)/shard_map/pallas_call | solution.py:319
  38.6 1.9 %copy.8 = f32[512,256]{1,0:T(8,128)} copy(f32[512,256]{1,0:T(8,128)} %shard_map.64) | data formatting | bytes 1048576
